TPU v7x, 128 devices: a whole 4x4x4 slice. The times are simulated.
128 devices in a mesh: row: 8 (over x_hi, z), col: 8 (over y, x_lo), layer: 2 (over core).
Axes of the slice: x: 4 (x_hi: 2, x_lo: 2; x = x_hi * 2 + x_lo), y: 4, z: 4, core: 2. Of those that a mesh axis runs over, the one named last changes fastest.
Arguments:
- expression: bfloat16 [24576, 1024], P(('row', 'col'), 'layer'), may hold values from -240 to 240
Outputs:
- connectivity: float32 [24576], P(('row', 'col', 'layer'))
All inputs are finite; a program needn't handle non-finite values.
Results may differ from a plain program's by a relative error of at most 0.00048.
Values may be sent and summed in bfloat16 or wider, within the bound.
No kernel may reach another device: no remote copies, remote signals or barrier semaphores. Data moves between devices by JAX's collectives and lax.ppermute only.
A program may use at most 64 MiB of HBM per device.

v0:
```python
import jax
import jax.numpy as jnp
from jax import lax
from jax.sharding import Mesh
from jax.sharding import PartitionSpec as P

S = 1024
COL = ("col_0", "col_1")
COL_LAYER = ("col_0", "col_1", "layer")
ROW_COL = ("row", "col_0", "col_1")
ROW_COL_LAYER = ("row", "col_0", "col_1", "layer")
epsilon = 1e-05


def whole_of(value, axes, dim):
    whole = value
    for number in range(len(axes) - 1, -1, -1):
        whole = lax.all_gather(whole, axes[number], axis=dim, tiled=True)
    return whole


def cut_along(value, dim, length):
    before, after = (value.shape[:dim], value.shape[dim + 1 :])
    return jnp.moveaxis(value.reshape(*before, length, -1, *after), dim, 0)


def sum_at_owner(value, axis, dim):
    length = lax.axis_size(axis)
    blocks = lax.all_to_all(cut_along(value, dim, length), axis, 0, 0, tiled=True)
    return jnp.sum(blocks, axis=0)


def adjacency(correlation):
    shifted = (1.0 + correlation) * 0.5
    square = shifted * shifted
    fourth = square * square
    eighth = fourth * fourth
    return eighth * fourth


def standardize(values, total, squares):
    average = total / S
    variance = squares / S - average * average
    return ((values - average[:, None]) * lax.rsqrt(variance + epsilon)[:, None]).astype(
        jnp.bfloat16
    )


def pair_products(left, right):
    return lax.dot_general(
        left, right, (((1,), (1,)), ((), ())), preferred_element_type=jnp.float32
    )


def on_device(expression):
    whole = lax.all_gather(expression, "layer", axis=1, tiled=True)
    values = whole.astype(jnp.float32)
    scaled = standardize(values, jnp.sum(values, axis=1), jnp.sum(values * values, axis=1))
    row_genes = whole_of(scaled, COL, 0)
    share = scaled.shape[0] // lax.axis_size("layer")
    own_half = lax.dynamic_slice_in_dim(scaled, lax.axis_index("layer") * share, share, 0)
    partial_value = jnp.sum(
        adjacency(
            pair_products(lax.all_gather(own_half, "row", axis=0, tiled=True), row_genes) / S
        ),
        axis=0,
    )
    summed = sum_at_owner(partial_value, COL_LAYER, 0)
    return summed - 1.0


def solution(mesh):
    torus = Mesh(
        mesh.devices.reshape(mesh.shape["row"], 4, 2, mesh.shape["layer"]),
        ("row", "col_0", "col_1", "layer"),
    )
    in_specs = (P(ROW_COL, "layer"),)
    out_specs = P(ROW_COL_LAYER)
    return jax.shard_map(
        on_device, mesh=torus, in_specs=in_specs, out_specs=out_specs, check_vma=False
    )
```

profile of v0, /device:TPU:1, one launch (start us, length us, event | category | flops | bytes accessed | tf_op | source)
XLA Modules:
  0.0 208.2 jit_solution(15841758606640467007)
XLA Ops:
  6.5 0.0 all-gather.6.cloned.1.call-start
  6.5 3.6 %all_gather.12 = bf16[384,1024]{1,0:T(8,128)(2,1)S(1)} all-gather(bf16[384,512]{1,0:T(8,128)(2,1)} %param.1), channel_id=1, replica_groups=mesh['row'=8,'col_0'=4,'col_1'=2,'layer'=2] {'layer'}, dimensions={1}, use_global_device_ids=true | all-gather | bytes 1179648 | tf_op jit(solution)/shard_map/all_gather | solution.py:56
  10.1 0.3 convert_reduce_fusion
  10.4 1.1 fusion.2
  11.6 0.0 all-gather.6.cloned.1.call-update
  11.6 0.0 all-gather.4.cloned.1.call-start
  11.7 1.8 constant_dynamic-slice_fusion
  13.4 0.0 all-gather.4.cloned.1.call-update
  13.5 0.0 all-gather.8.cloned.1.call-start
  13.5 30.0 %all-gather.6.cloned.1.call-done = bf16[768,1024]{1,0:T(8,128)(2,1)} async-done(((bf16[384,1024]{1,0:T(8,128)(2,1)}), bf16[768,1024]{1,0:T(8,128)(2,1)}) %all-gather.6.cloned.1.call-update) | async-done | bytes 1572880 | tf_op jit(solution)/shard_map/all_gather | solution.py:18
  43.5 0.0 all-gather.8.cloned.1.call-update
  43.5 65.1 %all-gather.4.cloned.1.call-done = bf16[1536,1024]{1,0:T(8,128)(2,1)} async-done(((bf16[192,1024]{1,0:T(8,128)(2,1)}), bf16[1536,1024]{1,0:T(8,128)(2,1)}) %all-gather.4.cloned.1.call-update) | async-done | bytes 3145744 | tf_op jit(solution)/shard_map/all_gather | solution.py:64
  108.6 65.7 %all-gather.8.cloned.1.call-done = bf16[3072,1024]{1,0:T(8,128)(2,1)} async-done(((bf16[768,1024]{1,0:T(8,128)(2,1)}), bf16[3072,1024]{1,0:T(8,128)(2,1)}) %all-gather.8.cloned.1.call-update) | async-done | bytes 6291472 | tf_op jit(solution)/shard_map/all_gather | solution.py:18
  174.3 15.7 %fusion = f32[3072]{0:T(1024)S(1)} fusion(bf16[1536,1024]{1,0:T(8,128)(2,1)} %all-gather.4.cloned.1.call-done, bf16[3072,1024]{1,0:T(8,128)(2,1)} %all-gather.8.cloned.1.call-done), kind=kOutput, calls=%fused_computation.1 | convolution fusion | flops 9701422080 | bytes 9449472 | tf_op jit(solution)/shard_map/dot_general | solution.py:50
  190.0 0.1 all_to_all.6
  190.1 11.0 %all_to_all.9 = f32[16,1,192]{2,1,0:T(1,128)S(1)} all-to-all(f32[16,1,192]{2,1,0:T(1,128)S(1)} %all_to_all.6), channel_id=1, replica_groups=mesh['row'=8,'col_0'=4,'col_1'=2,'layer'=2] {'col_0','col_1','layer'}, dimensions={0} | all-to-all | bytes 24576 | tf_op jit(solution)/shard_map/all_to_all | solution.py:29
  201.1 0.6 broadcast_add_fusion
  (2 shorter events, 0.0 us)
Async XLA Ops:
  6.5 36.9 %all-gather.6.cloned.1.call-start = ((), (), s32[]{:S(2)}) async-start(), calls=%async_computation.2 | async-start | bytes 2359296 | tf_op jit(solution)/shard_map/all_gather | solution.py:18
  11.6 97.0 %all-gather.4.cloned.1.call-start = ((), (), s32[]{:S(2)}) async-start(), calls=%async_computation.1 | async-start | bytes 3538944 | tf_op jit(solution)/shard_map/all_gather | solution.py:64
  13.5 160.9 %all-gather.8.cloned.1.call-start = ((), (), s32[]{:S(2)}) async-start(), calls=%async_computation.3 | async-start | bytes 7864320 | tf_op jit(solution)/shard_map/all_gather | solution.py:18
Sparse Core Ops, SparseCore 0:
  11.7 31.7 all-gather.5
  45.8 62.8 all-gather.3
  110.3 63.9 all-gather.7
where the time goes:
time: 208 us
  waiting for transfers between devices  161 us (77%)
  matrix products  15.7 us (8%)
  blocking collectives  14.6 us (7%)
  between operations  13.1 us (6%)
    all_gather x2, waiting for transfers between devices, whole_of(): whole = lax.all_gather(whole, axes[number], axis=dim, tiled=True)  95.6 us
    all_gather x1, waiting for transfers between devices, on_device(): lax.all_gather(own_half, 'row', axis=0, tiled=True)  65.1 us
    dot_general x1, matrix products, pair_products(): lax.dot_general(left, right, (((1,), (1,)), ((), ())), preferred_element_...  15.7 us
    all_to_all x1, blocking collectives, sum_at_owner(): lax.all_to_all(cut_along(value, dim, length), axis, 0, 0, tiled=True)  11 us
  transfers between devices with their start and end apart: 3, of which 3 were waited for; matrix products, arithmetic and copies ran while one was open for 1% of the time, Pallas kernels for 0%

commit v1 on v0

--- a/solution.py
+++ b/solution.py
@@ -10,6 +10,13 @@
 ROW_COL = ("row", "col_0", "col_1")
 ROW_COL_LAYER = ("row", "col_0", "col_1", "layer")
 epsilon = 1e-05
+
+
+def carry_the_forms(body, axis_tag, axis_k):
+    local_now = jnp.concatenate(
+        lax.all_to_all(jnp.stack([body] * lax.axis_size(axis_tag), 0), axis_tag, 0, 0), axis_k
+    )
+    return local_now
 
 
 def whole_of(value, axes, dim):
@@ -60,10 +67,7 @@
     share = scaled.shape[0] // lax.axis_size("layer")
     own_half = lax.dynamic_slice_in_dim(scaled, lax.axis_index("layer") * share, share, 0)
     partial_value = jnp.sum(
-        adjacency(
-            pair_products(lax.all_gather(own_half, "row", axis=0, tiled=True), row_genes) / S
-        ),
-        axis=0,
+        adjacency(pair_products(carry_the_forms(own_half, "row", 0), row_genes) / S), axis=0
     )
     summed = sum_at_owner(partial_value, COL_LAYER, 0)
     return summed - 1.0

time: 208 us -> 145 us (0.70)
  waiting for transfers between devices: 161 us -> 54.7 us
  blocking collectives: 14.6 us -> 58.6 us
    all_gather x1 -> x0, waiting for transfers between devices: 65.1 us -> none  [on_device(): lax.all_gather(own_half, 'row', axis=0, tiled=True)]
    all_to_all x0 -> x1, blocking collectives: none -> 44 us  [carry_the_forms(): lax.all_to_all(jnp.stack([body] * lax.axis_size(axis_tag), 0), axis_tag,...]
    all_gather x2, waiting for transfers between devices: 95.6 us -> 54.7 us  [whole_of(): whole = lax.all_gather(whole, axes[number], axis=dim, tiled=True)]
  transfers between devices with their start and end apart: 3 -> 2, of which waited for: 3 -> 2; matrix products, arithmetic and copies ran while one was open for 1% -> 1% of each run, Pallas kernels for 0% -> 0%
where the time goes in v1:
time: 145 us
  blocking collectives  58.6 us (40%)
  waiting for transfers between devices  54.7 us (38%)
  matrix products  14.7 us (10%)
  between operations  13.4 us (9%)
  other arithmetic  2.12 us (1%)
  local copies, waits for them, and re-layouts  1.5 us (1%)
    all_gather x2, waiting for transfers between devices, whole_of(): whole = lax.all_gather(whole, axes[number], axis=dim, tiled=True)  54.7 us
    all_to_all x1, blocking collectives, carry_the_forms(): lax.all_to_all(jnp.stack([body] * lax.axis_size(axis_tag), 0), axis_tag,...  44 us
    dot_general x1, matrix products, pair_products(): lax.dot_general(left, right, (((1,), (1,)), ((), ())), preferred_element_...  14.7 us
    all_to_all x1, blocking collectives, sum_at_owner(): lax.all_to_all(cut_along(value, dim, length), axis, 0, 0, tiled=True)  11 us
    all_gather x1, blocking collectives, on_device(): whole = lax.all_gather(expression, 'layer', axis=1, tiled=True)  3.58 us
  transfers between devices with their start and end apart: 2, of which 2 were waited for; matrix products, arithmetic and copies ran while one was open for 1% of the time, Pallas kernels for 0%

profile of v1, /device:TPU:1, one launch (start us, length us, event | category | flops | bytes accessed | tf_op | source)
XLA Modules:
  0.0 145.1 jit_solution(4109163026546437779)
XLA Ops:
  6.5 0.0 all-gather.3.cloned.1.call-start
  6.5 3.6 %all_gather.9 = bf16[384,1024]{1,0:T(8,128)(2,1)S(1)} all-gather(bf16[384,512]{1,0:T(8,128)(2,1)} %param.1), channel_id=1, replica_groups=mesh['row'=8,'col_0'=4,'col_1'=2,'layer'=2] {'layer'}, dimensions={1}, use_global_device_ids=true | all-gather | bytes 1179648 | tf_op jit(solution)/shard_map/all_gather | solution.py:63
  10.1 0.3 convert_reduce_fusion
  10.4 1.2 fusion.2
  11.6 0.0 all-gather.3.cloned.1.call-update
  11.7 0.0 all-gather.5.cloned.1.call-start
  11.7 31.8 %all-gather.3.cloned.1.call-done = bf16[768,1024]{1,0:T(8,128)(2,1)} async-done(((bf16[384,1024]{1,0:T(8,128)(2,1)}), bf16[768,1024]{1,0:T(8,128)(2,1)}) %all-gather.3.cloned.1.call-update) | async-done | bytes 1572880 | tf_op jit(solution)/shard_map/all_gather | solution.py:25
  43.5 0.0 all-gather.5.cloned.1.call-update
  43.6 1.0 constant_dynamic-slice_fusion
  44.6 0.4 stack.2
  45.0 44.0 %all_to_all.14 = bf16[8,192,1024]{2,1,0:T(8,128)(2,1)S(1)} all-to-all(bf16[8,192,1024]{2,1,0:T(8,128)(2,1)S(1)} %stack.2), channel_id=1, replica_groups=mesh['row'=8,'col_0'=4,'col_1'=2,'layer'=2] {'row'}, dimensions={0} | all-to-all | bytes 6291456 | tf_op jit(solution)/shard_map/all_to_all | solution.py:17
  89.0 22.9 %all-gather.5.cloned.1.call-done = bf16[3072,1024]{1,0:T(8,128)(2,1)} async-done(((bf16[768,1024]{1,0:T(8,128)(2,1)}), bf16[3072,1024]{1,0:T(8,128)(2,1)}) %all-gather.5.cloned.1.call-update) | async-done | bytes 6291472 | tf_op jit(solution)/shard_map/all_gather | solution.py:25
  111.9 14.7 %fusion = f32[3072]{0:T(1024)S(1)} fusion(bf16[1536,1024]{1,0:T(8,128)(2,1)S(1)} %bitcast.3, bf16[3072,1024]{1,0:T(8,128)(2,1)} %all-gather.5.cloned.1.call-done), kind=kOutput, calls=%fused_computation.1 | convolution fusion | flops 9701422080 | bytes 9449472 | tf_op jit(solution)/shard_map/dot_general | solution.py:57
  126.6 0.1 all_to_all.10
  126.7 11.0 %all_to_all.15 = f32[16,1,192]{2,1,0:T(1,128)S(1)} all-to-all(f32[16,1,192]{2,1,0:T(1,128)S(1)} %all_to_all.10), channel_id=1, replica_groups=mesh['row'=8,'col_0'=4,'col_1'=2,'layer'=2] {'col_0','col_1','layer'}, dimensions={0} | all-to-all | bytes 24576 | tf_op jit(solution)/shard_map/all_to_all | solution.py:36
  137.7 0.6 broadcast_add_fusion
  (2 shorter events, 0.0 us)
Async XLA Ops:
  6.5 37.0 %all-gather.3.cloned.1.call-start = ((), (), s32[]{:S(2)}) async-start(), calls=%async_computation.2 | async-start | bytes 2359296 | tf_op jit(solution)/shard_map/all_gather | solution.py:25
  11.7 100.2 %all-gather.5.cloned.1.call-start = ((), (), s32[]{:S(2)}) async-start(), calls=%async_computation.3 | async-start | bytes 7864320 | tf_op jit(solution)/shard_map/all_gather | solution.py:25
Sparse Core Ops, SparseCore 0:
  11.8 31.7 all-gather.2
  45.2 66.6 all-gather.4
